TPU v7x, 32 devices: a whole 2x2x4 slice. The times are simulated.
32 devices in a mesh: dp: 4 (over y, x), vocab: 8 (over z, core).
Axes of the slice: x: 2, y: 2, z: 4, core: 2. Of those that a mesh axis runs over, the one named last changes fastest.
Arguments:
- hidden: bfloat16 [512, 8192], P('dp', 'vocab'), may hold values from -20 to 20
- weight: bfloat16 [8192, 4752], P('dp', 'vocab'), may hold values from -0.198873782 to 0.198873782
- targets: int32 [512], P('dp'), may hold values from 0 to 4751
- loss_mask: int32 [512], P('dp'), may hold values 0 or 1
Outputs:
- grad_hidden: bfloat16 [512, 8192], P('dp', 'vocab')
- grad_weight: bfloat16 [8192, 4752], P('dp', 'vocab')
- token_loss: float32 [512], P('dp')
- grad_norm: float32 [], replicated
All inputs are finite; a program needn't handle non-finite values. No bound on the sum of `loss_mask` on one device may be relied on, other than what follows from the above.
Results may differ from a plain program's by a relative error of at most 0.0034.
Values may be sent and summed in bfloat16 or wider, within the bound.
A program may use at most 128 MiB of HBM per device.

v0:
```python
import jax
import jax.numpy as jnp
from jax import lax
from jax.sharding import PartitionSpec as P

loss_scale = 16.0


def on_device(hidden, weight, targets, loss_mask):
    shard_width = weight.shape[1]
    col_offset = lax.axis_index("vocab") * shard_width
    full_hidden = lax.all_gather(hidden, "vocab", axis=1, tiled=True)
    hidden_block = lax.all_to_all(full_hidden, "dp", split_axis=1, concat_axis=0, tiled=True)
    full_weight = lax.all_gather(weight, "dp", axis=0, tiled=True)
    logits = jnp.dot(full_hidden, full_weight, preferred_element_type=jnp.float32)
    row_targets, row_mask = (targets, loss_mask)
    local_col = row_targets - col_offset
    onehot = (lax.broadcasted_iota(jnp.int32, logits.shape, 1) == local_col[:, None]).astype(
        jnp.float32
    )
    target_local = jnp.sum(logits * onehot, axis=1)
    local_top = jnp.max(logits, axis=1)
    row_top = lax.pmax(local_top, "vocab")
    local_sum = jnp.sum(jnp.exp(logits - row_top[:, None]), axis=1)
    exp_sum, target_logit = lax.psum((local_sum, target_local), "vocab")
    log_total = row_top + jnp.log(exp_sum)
    row_keep = row_mask.astype(jnp.float32)
    loss_rows = row_keep * (log_total - target_logit)
    softmax = jnp.exp(logits - log_total[:, None])
    dlogits = (loss_scale * row_keep[:, None] * (softmax - onehot)).astype(jnp.bfloat16)
    dlog_all = lax.all_gather(dlogits, "dp", axis=0, tiled=True)
    hidden_terms = lax.dot_general(
        dlogits, full_weight, (((1,), (1,)), ((), ())), preferred_element_type=jnp.float32
    )
    hidden_grad_full = lax.psum_scatter(hidden_terms, "vocab", scatter_dimension=1, tiled=True)
    weight_grad_full = lax.dot_general(
        hidden_block, dlog_all, (((0,), (0,)), ((), ())), preferred_element_type=jnp.float32
    )
    local_squares = jnp.sum(weight_grad_full * weight_grad_full) + jnp.sum(
        hidden_grad_full * hidden_grad_full
    )
    squares_total = lax.psum(local_squares, ("dp", "vocab"))
    return (
        hidden_grad_full.astype(jnp.bfloat16),
        weight_grad_full.astype(jnp.bfloat16),
        loss_rows,
        jnp.sqrt(squares_total),
    )


def solution(mesh):
    placed = (P("dp", "vocab"), P("dp", "vocab"), P("dp"), P("dp"))
    return jax.shard_map(
        on_device,
        mesh=mesh,
        in_specs=placed,
        out_specs=(P("dp", "vocab"), P("dp", "vocab"), P("dp"), P()),
        check_vma=False,
    )
```

profile of v0, /device:TPU:12, one launch (start us, length us, event | category | flops | bytes accessed | tf_op | source)
XLA Modules:
  0.0 285.6 jit_solution(2477782353101069427)
XLA Ops:
  7.2 0.0 all-gather.3.cloned.1.call-start
  7.2 1.8 copy.8
  9.0 0.0 all-gather.3.cloned.1.call-update
  9.0 0.0 all-gather.5.cloned.1.call-start
  9.1 0.7 all-gather.5.cloned.1.call-update
  9.8 0.0 reduce-scatter.2.cloned.1.call-start
  9.9 30.6 %all-gather.3.cloned.1.call-done = bf16[128,8192]{0,1:T(8,128)(2,1)} async-done(((bf16[128,1024]{0,1:T(8,128)(2,1)}), bf16[128,8192]{0,1:T(8,128)(2,1)}) %all-gather.3.cloned.1.call-update) | async-done | bytes 2097168 | tf_op jit(solution)/shard_map/all_gather | solution.py:12
  40.4 100.8 %all-gather.5.cloned.1.call-done = bf16[8192,594]{0,1:T(8,128)(2,1)} async-done(((bf16[2048,594]{0,1:T(8,128)(2,1)}), bf16[8192,594]{0,1:T(8,128)(2,1)}) %all-gather.5.cloned.1.call-update) | async-done | bytes 9732112 | tf_op jit(solution)/shard_map/all_gather | solution.py:14
  141.2 6.2 %fusion = (f32[128]{0:T(128)S(1)}, f32[128,594]{0,1:T(8,128)S(1)}) fusion(bf16[128,8192]{0,1:T(8,128)(2,1)} %all-gather.3.cloned.1.call-done, bf16[8192,594]{0,1:T(8,128)(2,1)} %all-gather.5.cloned.1.call-done), kind=kOutput, calls=%fused_computation.11 | convolution fusion | flops 1245784192 | bytes 12133888 | tf_op jit(solution)/shard_map/dot_general | solution.py:15
  147.4 12.7 %pmax.7 = f32[128]{0:T(128)S(1)} all-reduce(f32[128]{0:T(128)S(1)} %get-tuple-element.15), channel_id=1, replica_groups=mesh['dp'=4,'vocab'=8] {'vocab'}, use_global_device_ids=true, to_apply=%region_1.0 | all-reduce | flops 128 | bytes 1024 | tf_op jit(solution)/shard_map/pmax | solution.py:23
  160.1 0.1 select_reduce_fusion
  160.2 13.6 %all-reduce = (f32[128]{0:T(128)S(1)}, f32[128]{0:T(128)S(1)}) all-reduce(f32[128]{0:T(128)S(1)} %get-tuple-element.5, f32[128]{0:T(128)S(1)} %get-tuple-element.4), channel_id=1, replica_groups=mesh['dp'=4,'vocab'=8] {'vocab'}, use_global_device_ids=true, to_apply=%region_3.0 | all-reduce | flops 256 | bytes 2048 | tf_op jit(solution)/shard_map/psum | solution.py:25
  173.8 0.5 subtract_multiply_fusion
  174.3 0.1 multiply_convert_fusion
  174.4 8.0 %fusion.1 = f32[128,8192]{1,0:T(8,128)} fusion(bf16[128,594]{0,1:T(8,128)(2,1)S(1)} %multiply_convert_fusion, bf16[8192,594]{0,1:T(8,128)(2,1)} %all-gather.5.cloned.1.call-done), kind=kOutput, calls=%fused_computation.12 | convolution fusion | flops 1245708288 | bytes 14078464 | tf_op jit(solution)/shard_map/dot_general | solution.py:32
  182.4 0.0 reduce-scatter.2.cloned.1.call-update
  182.4 1.6 copy-done
  184.0 28.4 %all_to_all.19 = bf16[128,4,2048]{0,2,1:T(8,128)(2,1)} all-to-all(bf16[128,4,2048]{0,2,1:T(8,128)(2,1)S(1)} %bitcast.11), channel_id=1, replica_groups=mesh['dp'=4,'vocab'=8] {'dp'}, dimensions={1} | all-to-all | bytes 4194304 | tf_op jit(solution)/shard_map/all_to_all | solution.py:13
  212.3 2.9 %copy.9 = bf16[4,128,2048]{2,1,0:T(8,128)(2,1)S(1)} copy(bf16[4,128,2048]{1,2,0:T(8,128)(2,1)} %bitcast.12) | data formatting | bytes 4194304 | tf_op jit(solution)/shard_map/all_to_all | solution.py:13
  215.3 10.0 %all_gather.11 = bf16[512,594]{0,1:T(8,128)(2,1)S(1)} all-gather(bf16[128,594]{0,1:T(8,128)(2,1)S(1)} %multiply_convert_fusion), channel_id=1, replica_groups=mesh['dp'=4,'vocab'=8] {'dp'}, dimensions={0}, use_global_device_ids=true | all-gather | bytes 760320 | tf_op jit(solution)/shard_map/all_gather | solution.py:31
  225.3 3.6 %multiply_reduce_fusion = (f32[]{:T(128)}, bf16[2048,594]{0,1:T(8,128)(2,1)}) fusion(bf16[512,594]{0,1:T(8,128)(2,1)S(1)} %all_gather.11, bf16[512,2048]{1,0:T(8,128)(2,1)S(1)} %bitcast.13), kind=kOutput, calls=%fused_computation | convolution fusion | flops 1249357824 | bytes 5138436 | tf_op jit(solution)/shard_map/dot_general | solution.py:36
  228.9 1.2 reduce-scatter.2.cloned.1.call-done
  230.1 2.6 multiply_reduce_fusion.1
  234.0 43.3 %psum.23 = f32[]{:T(128)} all-reduce(f32[]{:T(128)S(6)} %add.15), channel_id=1, replica_groups=mesh['dp'=4,'vocab'=8] {'dp','vocab'}, use_global_device_ids=true, to_apply=%region_9.0 | all-reduce | flops 1 | bytes 8 | tf_op jit(solution)/shard_map/psum | solution.py:42
  (6 shorter events, 0.0 us)
Async XLA Ops:
  7.2 2.7 copy-start.2
  7.2 33.3 %all-gather.3.cloned.1.call-start = ((), (), s32[]{:S(2)}) async-start(), calls=%async_computation.2 | async-start | bytes 2359296 | tf_op jit(solution)/shard_map/all_gather | solution.py:12
  9.0 132.2 %all-gather.5.cloned.1.call-start = ((), (), s32[]{:S(2)}) async-start(), calls=%async_computation.3 | async-start | bytes 12288000 | tf_op jit(solution)/shard_map/all_gather | solution.py:14
  9.8 220.3 %reduce-scatter.2.cloned.1.call-start = ((), (), s32[]{:S(2)}) async-start(), calls=%async_computation.4 | async-start | bytes 4718592 | tf_op jit(solution)/shard_map/reduce_scatter | solution.py:35
  9.9 163.9 %copy-start.1 = (s32[128]{0:T(128)S(1)}, s32[128]{0:T(128)}, u32[]{:S(2)}) copy-start(s32[128]{0:T(128)} %param.7) | copy-start | bytes 1540
  182.4 1.6 copy-start
Sparse Core Ops, SparseCore 0:
  10.2 30.2 all-gather.2
  42.3 98.8 all-gather.4
  182.5 47.5 reduce-scatter.1
where the time goes:
time: 286 us
  waiting for transfers between devices  133 us (47%)
  blocking collectives  108 us (38%)
  matrix products  17.8 us (6%)
  between operations  17 us (6%)
  local copies, waits for them, and re-layouts  6.31 us (2%)
  other arithmetic  3.29 us (1%)
    all_gather x1, waiting for transfers between devices, on_device(): full_weight = lax.all_gather(weight, 'dp', axis=0, tiled=True)  101 us
    psum x1, blocking collectives, on_device(): squares_total = lax.psum(local_squares, ('dp', 'vocab'))  43.3 us
    all_gather x1, waiting for transfers between devices, on_device(): full_hidden = lax.all_gather(hidden, 'vocab', axis=1, tiled=True)  30.6 us
    all_to_all x1, blocking collectives, on_device(): lax.all_to_all(full_hidden, 'dp', split_axis=1, concat_axis=0, tiled=True)  28.4 us
    psum x1, blocking collectives, on_device(): exp_sum, target_logit = lax.psum((local_sum, target_local), 'vocab')  13.6 us
    pmax x1, blocking collectives, on_device(): row_top = lax.pmax(local_top, 'vocab')  12.7 us
    all_gather x1, blocking collectives, on_device(): dlog_all = lax.all_gather(dlogits, 'dp', axis=0, tiled=True)  10 us
    dot_general x1, matrix products, on_device(): lax.dot_general(dlogits, full_weight, (((1,), (1,)), ((), ())), preferred...  8.01 us
  transfers between devices with their start and end apart: 3, of which 3 were waited for; matrix products, arithmetic and copies ran while one was open for 2% of the time, Pallas kernels for 0%

commit v1 on v0

--- a/solution.py
+++ b/solution.py
@@ -9,7 +9,7 @@
 def on_device(hidden, weight, targets, loss_mask):
     shard_width = weight.shape[1]
     col_offset = lax.axis_index("vocab") * shard_width
-    full_hidden = lax.all_gather(hidden, "vocab", axis=1, tiled=True)
+    full_hidden = jnp.concatenate(lax.all_gather(hidden, "vocab"), axis=1)
     hidden_block = lax.all_to_all(full_hidden, "dp", split_axis=1, concat_axis=0, tiled=True)
     full_weight = lax.all_gather(weight, "dp", axis=0, tiled=True)
     logits = jnp.dot(full_hidden, full_weight, preferred_element_type=jnp.float32)

time: 286 us -> 285 us (level)
    unnamed x7 -> x4, local copies, waits for them, and re-layouts: 3.37 us -> 0.01 us
    all_gather x1, waiting for transfers between devices: 101 us -> 97.7 us  [on_device(): full_weight = lax.all_gather(weight, 'dp', axis=0, tiled=True)]
    reshape x0 -> x1, local copies, waits for them, and re-layouts: none -> 3.03 us  [on_device(): full_hidden = jnp.concatenate(lax.all_gather(hidden, 'vocab'), axis=1)]
  transfers between devices with their start and end apart: 3 -> 3, of which waited for: 3 -> 3; matrix products, arithmetic and copies ran while one was open for 2% -> 3% of each run, Pallas kernels for 0% -> 0%
where the time goes in v1:
time: 285 us; the launch traced here: 284 us
  waiting for transfers between devices  133 us (47%)
  blocking collectives  108 us (38%)
  matrix products  17.1 us (6%)
  between operations  17 us (6%)
  local copies, waits for them, and re-layouts  5.97 us (2%)
  other arithmetic  3.29 us (1%)
    all_gather x1, waiting for transfers between devices, on_device(): full_weight = lax.all_gather(weight, 'dp', axis=0, tiled=True)  97.7 us
    psum x1, blocking collectives, on_device(): squares_total = lax.psum(local_squares, ('dp', 'vocab'))  43.3 us
    all_gather x1, waiting for transfers between devices, on_device(): full_hidden = jnp.concatenate(lax.all_gather(hidden, 'vocab'), axis=1)  31.1 us
    all_to_all x1, blocking collectives, on_device(): lax.all_to_all(full_hidden, 'dp', split_axis=1, concat_axis=0, tiled=True)  28.4 us
    psum x1, blocking collectives, on_device(): exp_sum, target_logit = lax.psum((local_sum, target_local), 'vocab')  13.6 us
    pmax x1, blocking collectives, on_device(): row_top = lax.pmax(local_top, 'vocab')  12.7 us
    all_gather x1, blocking collectives, on_device(): dlog_all = lax.all_gather(dlogits, 'dp', axis=0, tiled=True)  10 us
    dot_general x1, matrix products, on_device(): lax.dot_general(dlogits, full_weight, (((1,), (1,)), ((), ())), preferred...  8.01 us
  transfers between devices with their start and end apart: 3, of which 3 were waited for; matrix products, arithmetic and copies ran while one was open for 3% of the time, Pallas kernels for 0%

profile of v1, /device:TPU:12, one launch (start us, length us, event | category | flops | bytes accessed | tf_op | source)
XLA Modules:
  0.0 284.4 jit_solution(13133676767480511672)
XLA Ops:
  7.2 0.0 copy-start.1
  7.2 0.0 all-gather.6.cloned.1.call-start
  7.2 0.7 all-gather.6.cloned.1.call-update
  7.9 0.0 all-gather.4.cloned.1.call-start
  8.0 0.7 all-gather.4.cloned.1.call-update
  8.7 0.0 reduce-scatter.2.cloned.1.call-start
  8.7 31.1 %all-gather.6.cloned.1.call-done = bf16[1024,1024]{1,0:T(8,128)(2,1)} async-done(((bf16[128,1024]{1,0:T(8,128)(2,1)}), bf16[1024,1024]{1,0:T(8,128)(2,1)}) %all-gather.6.cloned.1.call-update) | async-done | bytes 2097168 | tf_op jit(solution)/shard_map/all_gather | solution.py:12
  39.9 3.0 %copy.9 = bf16[128,8,1024]{0,2,1:T(8,128)(2,1)S(1)} copy(bf16[128,8,1024]{2,0,1:T(8,128)(2,1)} %bitcast.18) | data formatting | bytes 4194304 | tf_op jit(solution)/shard_map/reshape | solution.py:12
  42.9 97.7 %all-gather.4.cloned.1.call-done = bf16[8192,594]{0,1:T(8,128)(2,1)} async-done(((bf16[2048,594]{0,1:T(8,128)(2,1)}), bf16[8192,594]{0,1:T(8,128)(2,1)}) %all-gather.4.cloned.1.call-update) | async-done | bytes 9732112 | tf_op jit(solution)/shard_map/all_gather | solution.py:14
  140.6 5.5 %fusion = (f32[128]{0:T(128)S(1)}, f32[128,594]{0,1:T(8,128)S(1)}) fusion(bf16[128,8192]{0,1:T(8,128)(2,1)S(1)} %bitcast.15, bf16[8192,594]{0,1:T(8,128)(2,1)} %all-gather.4.cloned.1.call-done), kind=kOutput, calls=%fused_computation.11 | convolution fusion | flops 1245784192 | bytes 12133888 | tf_op jit(solution)/shard_map/dot_general | solution.py:15
  146.1 12.7 %pmax.7 = f32[128]{0:T(128)S(1)} all-reduce(f32[128]{0:T(128)S(1)} %get-tuple-element.15), channel_id=1, replica_groups=mesh['dp'=4,'vocab'=8] {'vocab'}, use_global_device_ids=true, to_apply=%region_1.0 | all-reduce | flops 128 | bytes 1024 | tf_op jit(solution)/shard_map/pmax | solution.py:23
  158.8 0.1 select_reduce_fusion
  158.9 13.6 %all-reduce = (f32[128]{0:T(128)S(1)}, f32[128]{0:T(128)S(1)}) all-reduce(f32[128]{0:T(128)S(1)} %get-tuple-element.5, f32[128]{0:T(128)S(1)} %get-tuple-element.4), channel_id=1, replica_groups=mesh['dp'=4,'vocab'=8] {'vocab'}, use_global_device_ids=true, to_apply=%region_3.0 | all-reduce | flops 256 | bytes 2048 | tf_op jit(solution)/shard_map/psum | solution.py:25
  172.5 0.5 subtract_multiply_fusion
  173.0 0.1 multiply_convert_fusion
  173.1 8.0 %fusion.1 = f32[128,8192]{1,0:T(8,128)} fusion(bf16[128,594]{0,1:T(8,128)(2,1)S(1)} %multiply_convert_fusion, bf16[8192,594]{0,1:T(8,128)(2,1)} %all-gather.4.cloned.1.call-done), kind=kOutput, calls=%fused_computation.12 | convolution fusion | flops 1245708288 | bytes 14078464 | tf_op jit(solution)/shard_map/dot_general | solution.py:32
  181.1 0.0 reduce-scatter.2.cloned.1.call-update
  181.2 28.4 %all_to_all.19 = bf16[128,4,2048]{0,2,1:T(8,128)(2,1)} all-to-all(bf16[128,4,2048]{0,2,1:T(8,128)(2,1)S(1)} %bitcast.16), channel_id=1, replica_groups=mesh['dp'=4,'vocab'=8] {'dp'}, dimensions={1} | all-to-all | bytes 4194304 | tf_op jit(solution)/shard_map/all_to_all | solution.py:13
  209.5 2.9 %copy.11 = bf16[4,128,2048]{2,1,0:T(8,128)(2,1)S(1)} copy(bf16[4,128,2048]{1,2,0:T(8,128)(2,1)} %bitcast.17) | data formatting | bytes 4194304 | tf_op jit(solution)/shard_map/all_to_all | solution.py:13
  212.5 10.0 %all_gather.15 = bf16[512,594]{0,1:T(8,128)(2,1)S(1)} all-gather(bf16[128,594]{0,1:T(8,128)(2,1)S(1)} %multiply_convert_fusion), channel_id=1, replica_groups=mesh['dp'=4,'vocab'=8] {'dp'}, dimensions={0}, use_global_device_ids=true | all-gather | bytes 760320 | tf_op jit(solution)/shard_map/all_gather | solution.py:31
  222.5 3.6 %multiply_reduce_fusion = (f32[]{:T(128)}, bf16[2048,594]{0,1:T(8,128)(2,1)}) fusion(bf16[512,594]{0,1:T(8,128)(2,1)S(1)} %all_gather.15, bf16[512,2048]{1,0:T(8,128)(2,1)S(1)} %bitcast.19), kind=kOutput, calls=%fused_computation | convolution fusion | flops 1249357824 | bytes 5138436 | tf_op jit(solution)/shard_map/dot_general | solution.py:36
  226.1 2.8 reduce-scatter.2.cloned.1.call-done
  228.9 2.6 multiply_reduce_fusion.1
  232.8 43.3 %psum.23 = f32[]{:T(128)} all-reduce(f32[]{:T(128)S(6)} %add.15), channel_id=1, replica_groups=mesh['dp'=4,'vocab'=8] {'dp','vocab'}, use_global_device_ids=true, to_apply=%region_9.0 | all-reduce | flops 1 | bytes 8 | tf_op jit(solution)/shard_map/psum | solution.py:42
  (4 shorter events, 0.0 us)
Async XLA Ops:
  7.2 1.5 copy-start.1
  7.2 32.7 %all-gather.6.cloned.1.call-start = ((), (), s32[]{:S(2)}) async-start(), calls=%async_computation.4 | async-start | bytes 2359296 | tf_op jit(solution)/shard_map/all_gather | solution.py:12
  7.9 132.7 %all-gather.4.cloned.1.call-start = ((), (), s32[]{:S(2)}) async-start(), calls=%async_computation.2 | async-start | bytes 12288000 | tf_op jit(solution)/shard_map/all_gather | solution.py:14
  8.7 220.2 %reduce-scatter.2.cloned.1.call-start = ((), (), s32[]{:S(2)}) async-start(), calls=%async_computation.3 | async-start | bytes 4718592 | tf_op jit(solution)/shard_map/reduce_scatter | solution.py:35
  140.6 31.9 %copy-start = (s32[128]{0:T(128)S(1)}, s32[128]{0:T(128)}, u32[]{:S(2)}) copy-start(s32[128]{0:T(128)} %param.7) | copy-start | bytes 1540
Sparse Core Ops, SparseCore 0:
  9.6 30.2 all-gather.5
  41.7 98.8 all-gather.3
  181.3 47.5 reduce-scatter.1
